TPU v7x, 32 devices: a whole 2x2x4 slice. The times are simulated.
32 devices in a mesh: dp: 8 (over y, x, core), expert: 4 (over z).
Axes of the slice: x: 2, y: 2, z: 4, core: 2. Of those that a mesh axis runs over, the one named last changes fastest.
Arguments:
- hidden_act: bfloat16 [4096, 2048], P('dp', 'expert'), may hold values from -6 to 6
- out_grad: bfloat16 [4096, 7168], P('dp'), may hold values from -0.125 to 0.125
- counts: int32 [8], P('dp'), may hold values from 0 to 512
- expert_master: float32 [7168, 2048], P('dp', 'expert'), may hold values from -0.005 to 0.005
- expert_mom: float32 [7168, 2048], P('dp', 'expert'), may hold values from -0.12 to 0.12
- expert_var: float32 [7168, 2048], P('dp', 'expert'), may hold values from 0.001 to 0.1
- dense_partial: float32 [8, 4, 14336], P('dp', 'expert'), may hold values from -0.8 to 0.8
- dense_master: float32 [14336], replicated, may hold values from 0.5 to 1.5
- dense_mom: float32 [14336], replicated, may hold values from -2 to 2
- dense_var: float32 [14336], replicated, may hold values from 0.1 to 10
Outputs:
- routed_weight: bfloat16 [7168, 2048], P(None, 'expert')
- new_expert_master: float32 [7168, 2048], P('dp', 'expert')
- new_expert_mom: float32 [7168, 2048], P('dp', 'expert')
- new_expert_var: float32 [7168, 2048], P('dp', 'expert')
- new_dense_master: float32 [14336], replicated
- new_dense_mom: float32 [14336], replicated
- new_dense_var: float32 [14336], replicated
All inputs are finite; a program needn't handle non-finite values.
Results may differ from a plain program's by a relative error of at most 0.0004.
Values may be sent and summed in bfloat16 or wider, within the bound.
No kernel may reach another device: no remote copies, remote signals or barrier semaphores. Data moves between devices by JAX's collectives and lax.ppermute only.
A program may use at most 128 MiB of HBM per device.

v0:
```python
import jax
import jax.numpy as jnp
from jax import lax
from jax.sharding import PartitionSpec as P

beta_one = 0.9
beta_two = 0.95
learn_rate = 0.00022
decay_rate = 0.1
epsilon = 1e-08
step_count = 100


def adamw(gradient, master, moment, second):
    moment_new = beta_one * moment + (1.0 - beta_one) * gradient
    second_new = beta_two * second + (1.0 - beta_two) * gradient * gradient
    first_fix = 1.0 - beta_one**step_count
    second_fix = 1.0 - beta_two**step_count
    update = (
        moment_new / first_fix / (jnp.sqrt(second_new / second_fix) + epsilon) + decay_rate * master
    )
    return (master - learn_rate * update, moment_new, second_new)


def on_device(
    hidden_act,
    out_grad,
    counts,
    expert_master,
    expert_mom,
    expert_var,
    dense_partial,
    dense_master,
    dense_mom,
    dense_var,
):
    slots = hidden_act.shape[0]
    row_live = lax.iota(jnp.int32, slots) < counts[0]
    masked = jnp.where(row_live[:, None], hidden_act, jnp.zeros_like(hidden_act))
    dense_local = dense_partial.reshape(-1)
    expert_grad = lax.psum_scatter(
        lax.dot_general(
            out_grad, masked, (((0,), (0,)), ((), ())), preferred_element_type=jnp.float32
        ),
        "dp",
        scatter_dimension=0,
        tiled=True,
    )
    dense_grad = lax.psum(dense_local, ("dp", "expert"))
    dense_new, dense_moment, dense_second = adamw(dense_grad, dense_master, dense_mom, dense_var)
    master_new, moment_new, second_new = adamw(expert_grad, expert_master, expert_mom, expert_var)
    routed_weight = lax.all_gather(master_new.astype(jnp.bfloat16), "dp", axis=0, tiled=True)
    return (
        routed_weight,
        master_new,
        moment_new,
        second_new,
        dense_new,
        dense_moment,
        dense_second,
    )


def solution(mesh):
    in_specs = (
        P("dp", "expert"),
        P("dp", None),
        P("dp"),
        P("dp", "expert"),
        P("dp", "expert"),
        P("dp", "expert"),
        P("dp", "expert", None),
        P(),
        P(),
        P(),
    )
    out_specs = (
        P(None, "expert"),
        P("dp", "expert"),
        P("dp", "expert"),
        P("dp", "expert"),
        P(),
        P(),
        P(),
    )
    return jax.shard_map(
        on_device, mesh=mesh, in_specs=in_specs, out_specs=out_specs, check_vma=False
    )
```

profile of v0, /device:TPU:0, one launch (start us, length us, event | category | flops | bytes accessed | tf_op | source)
XLA Modules:
  0.0 200.4 jit_solution(5589663375833429149)
XLA Ops:
  7.2 0.0 reduce-scatter.2.cloned.1.call-start
  7.9 12.6 %convolution_bitcast_fusion = f32[7168,512]{0,1:T(8,128)} fusion(bf16[512,7168]{1,0:T(8,128)(2,1)} %param.11, bf16[512,512]{1,0:T(8,128)(2,1)} %param.10, pred[512]{0:T(512)(128)(4,1)S(1)} %iota_compare_fusion), kind=kOutput, calls=%fused_computation | convolution fusion | flops 3758358528 | bytes 22544896 | tf_op jit(solution)/shard_map/dot_general | solution.py:42
  20.5 0.0 copy-start
  20.5 0.0 reduce-scatter.2.cloned.1.call-update
  20.5 0.0 all-gather.2.cloned.1.call-start
  20.5 1.4 copy-done
  22.0 1.7 copy.17
  23.6 2.9 %copy.18 = f32[896,512]{0,1:T(8,128)} copy(f32[896,512]{1,0:T(8,128)} %param.15) | data formatting | bytes 3670016 | tf_op args[5]
  26.5 0.0 copy-done.1
  26.5 1.7 copy.20
  28.2 97.5 %reduce-scatter.2.cloned.1.call-done = f32[896,512]{0,1:T(8,128)} async-done(((f32[7168,512]{0,1:T(8,128)}), f32[896,512]{0,1:T(8,128)}) %reduce-scatter.2.cloned.1.call-update) | async-done | bytes 1835024 | tf_op jit(solution)/shard_map/reduce_scatter | solution.py:41
  125.6 6.9 %fusion.7 = (bf16[896,512]{0,1:T(8,128)(2,1)}, f32[896,512]{0,1:T(8,128)}, f32[896,512]{0,1:T(8,128)}, f32[896,512]{0,1:T(8,128)S(1)}) fusion(f32[896,512]{0,1:T(8,128)} %copy.20, f32[896,512]{0,1:T(8,128)} %reduce-scatter.2.cloned.1.call-done, f32[896,512]{0,1:T(8,128)} %copy.17, f32[896,512]{0,1:T(8,128)} %copy.18), kind=kLoop, calls=%fused_computation.14 | loop fusion | flops 7340032 | bytes 13762560 | tf_op jit(solution)/shard_map/convert_element_type | solution.py:52
  132.5 0.0 all-gather.2.cloned.1.call-update
  132.5 0.0 copy-done.5
  132.6 40.8 %psum.7 = f32[14336]{0:T(1024)S(1)} all-reduce(f32[14336]{0:T(1024)S(1)} %bitcast.6), channel_id=1, replica_groups=mesh['dp'=8,'expert'=4] {'dp','expert'}, use_global_device_ids=true, to_apply=%region_1.2 | all-reduce | flops 14336 | bytes 114688 | tf_op jit(solution)/shard_map/psum | solution.py:49
  173.3 0.0 copy-done.2
  173.3 0.0 copy-done.3
  173.3 0.0 copy-done.4
  173.3 0.7 multiply_subtract_fusion.1
  174.0 2.7 %copy.22 = f32[896,512]{1,0:T(8,128)} copy(f32[896,512]{0,1:T(8,128)} %get-tuple-element.18) | data formatting | bytes 3670016
  176.8 2.7 %copy.23 = f32[896,512]{1,0:T(8,128)} copy(f32[896,512]{0,1:T(8,128)} %get-tuple-element.19) | data formatting | bytes 3670016
  179.5 1.7 copy.24
  181.1 2.0 all-gather.2.cloned.1.call-done
  183.1 10.4 %copy.21 = bf16[7168,512]{1,0:T(8,128)(2,1)} copy(bf16[7168,512]{0,1:T(8,128)(2,1)} %all-gather.2.cloned.1.call-done) | data formatting | bytes 14680064
  (6 shorter events, 0.0 us)
Async XLA Ops:
  7.2 118.5 %reduce-scatter.2.cloned.1.call-start = ((), (), s32[]{:S(2)}) async-start(), calls=%async_computation.1 | async-start | bytes 16515072 | tf_op jit(solution)/shard_map/reduce_scatter | solution.py:41
  20.5 1.5 copy-start
  20.5 162.6 %all-gather.2.cloned.1.call-start = ((), (), s32[]{:S(2)}) async-start(), calls=%async_computation.2 | async-start | bytes 8257536 | tf_op jit(solution)/shard_map/all_gather | solution.py:52
  23.6 2.9 %copy-start.1 = (f32[896,512]{1,0:T(8,128)S(1)}, f32[896,512]{1,0:T(8,128)}, u32[]{:S(2)}) copy-start(f32[896,512]{1,0:T(8,128)} %param.13) | copy-start | bytes 5505028
  28.2 104.4 %copy-start.5 = (f32[1,1,14336]{2,1,0:T(1,128)S(1)}, f32[1,1,14336]{2,1,0:T(1,128)}, u32[]{:S(2)}) copy-start(f32[1,1,14336]{2,1,0:T(1,128)} %param.16) | copy-start | bytes 172036
  28.2 145.2 %copy-start.2 = (f32[14336]{0:T(1024)S(1)}, f32[14336]{0:T(1024)}, u32[]{:S(2)}) copy-start(f32[14336]{0:T(1024)} %param.17) | copy-start | bytes 172036
  28.2 145.2 %copy-start.3 = (f32[14336]{0:T(1024)S(1)}, f32[14336]{0:T(1024)}, u32[]{:S(2)}) copy-start(f32[14336]{0:T(1024)} %param.18) | copy-start | bytes 172036
  28.2 145.2 %copy-start.4 = (f32[14336]{0:T(1024)S(1)}, f32[14336]{0:T(1024)}, u32[]{:S(2)}) copy-start(f32[14336]{0:T(1024)} %param.19) | copy-start | bytes 172036
Sparse Core Ops, SparseCore 0:
  20.6 104.9 reduce-scatter.1
  132.7 50.4 all-gather.1
where the time goes:
time: 201 us; the launch traced here: 200 us
  waiting for transfers between devices  99.5 us (50%)
  blocking collectives  40.8 us (20%)
  local copies, waits for them, and re-layouts  25.2 us (13%)
  between operations  14.7 us (7%)
  matrix products  12.6 us (6%)
  other arithmetic  7.57 us (4%)
    reduce_scatter x1, waiting for transfers between devices, on_device(): lax.psum_scatter(lax.dot_general(out_grad, masked, (((0,), (0,)), ((), ()...  97.5 us
    psum x1, blocking collectives, on_device(): dense_grad = lax.psum(dense_local, ('dp', 'expert'))  40.8 us
    unnamed x19, local copies, waits for them, and re-layouts  25.2 us
    dot_general x1, matrix products, on_device(): lax.dot_general(out_grad, masked, (((0,), (0,)), ((), ())), preferred_ele...  12.6 us
    convert_element_type x1, other arithmetic, on_device(): master_new.astype(jnp.bfloat16)  6.88 us
  transfers between devices with their start and end apart: 2, of which 2 were waited for; matrix products, arithmetic and copies ran while one was open for 7% of the time, Pallas kernels for 0%

commit v1 on v0

--- a/solution.py
+++ b/solution.py
@@ -46,7 +46,8 @@
         scatter_dimension=0,
         tiled=True,
     )
-    dense_grad = lax.psum(dense_local, ("dp", "expert"))
+    parts = lax.all_gather(dense_local, ("dp", "expert"))
+    dense_grad = jnp.sum(parts, axis=0)
     dense_new, dense_moment, dense_second = adamw(dense_grad, dense_master, dense_mom, dense_var)
     master_new, moment_new, second_new = adamw(expert_grad, expert_master, expert_mom, expert_var)
     routed_weight = lax.all_gather(master_new.astype(jnp.bfloat16), "dp", axis=0, tiled=True)

time: 201 us -> 205 us (1.020)
  blocking collectives: 40.8 us -> 0 us
  waiting for transfers between devices: 99.5 us -> 140 us
  other arithmetic: 7.57 us -> 10.1 us
    psum x1 -> x0, blocking collectives: 40.8 us -> none  [on_device(): dense_grad = lax.psum(dense_local, ('dp', 'expert'))]
    all_gather x1, waiting for transfers between devices: 1.97 us -> 39 us  [on_device(): lax.all_gather(master_new.astype(jnp.bfloat16), 'dp', axis=0, tiled=True)]
    reduce_scatter x1, waiting for transfers between devices: 97.5 us -> 101 us  [on_device(): lax.psum_scatter(lax.dot_general(out_grad, masked, (((0,), (0,)), ((), ()...]
    reduce_sum x0 -> x1, other arithmetic: none -> 2.55 us  [on_device(): dense_grad = jnp.sum(parts, axis=0)]
    unnamed x19 -> x17, local copies, waits for them, and re-layouts: 25.2 us -> 24.7 us
  transfers between devices with their start and end apart: 2 -> 3, of which waited for: 2 -> 2; matrix products, arithmetic and copies ran while one was open for 7% -> 12% of each run, Pallas kernels for 0% -> 0%
where the time goes in v1:
time: 205 us; the launch traced here: 204 us
  waiting for transfers between devices  140 us (68%)
  local copies, waits for them, and re-layouts  24.7 us (12%)
  between operations  16.2 us (8%)
  matrix products  12.6 us (6%)
  other arithmetic  10.1 us (5%)
    reduce_scatter x1, waiting for transfers between devices, on_device(): lax.psum_scatter(lax.dot_general(out_grad, masked, (((0,), (0,)), ((), ()...  101 us
    all_gather x1, waiting for transfers between devices, on_device(): lax.all_gather(master_new.astype(jnp.bfloat16), 'dp', axis=0, tiled=True)  39 us
    unnamed x17, local copies, waits for them, and re-layouts  24.7 us
    dot_general x1, matrix products, on_device(): lax.dot_general(out_grad, masked, (((0,), (0,)), ((), ())), preferred_ele...  12.6 us
    convert_element_type x1, other arithmetic, on_device(): master_new.astype(jnp.bfloat16)  6.89 us
  transfers between devices with their start and end apart: 3, of which 2 were waited for; matrix products, arithmetic and copies ran while one was open for 12% of the time, Pallas kernels for 0%

profile of v1, /device:TPU:0, one launch (start us, length us, event | category | flops | bytes accessed | tf_op | source)
XLA Modules:
  0.0 204.2 jit_solution(8898652529132397248)
XLA Ops:
  8.0 0.0 reduce-scatter.2.cloned.1.call-start
  8.7 12.6 %convolution_bitcast_fusion = f32[7168,512]{0,1:T(8,128)} fusion(bf16[512,7168]{1,0:T(8,128)(2,1)} %param.11, bf16[512,512]{1,0:T(8,128)(2,1)} %param.10, pred[512]{0:T(512)(128)(4,1)S(1)} %iota_compare_fusion), kind=kOutput, calls=%fused_computation | convolution fusion | flops 3758358528 | bytes 22544896 | tf_op jit(solution)/shard_map/dot_general | solution.py:42
  21.3 0.0 reduce-scatter.2.cloned.1.call-update
  21.3 0.0 all-gather.6.cloned.1.call-start
  21.4 0.5 all-gather.6.cloned.1.call-update
  21.9 0.0 all-gather.4.cloned.1.call-start
  21.9 0.8 copy-done
  22.8 1.7 copy.25
  24.5 2.9 %copy.26 = f32[896,512]{0,1:T(8,128)} copy(f32[896,512]{1,0:T(8,128)} %param.15) | data formatting | bytes 3670016 | tf_op args[5]
  27.3 0.0 copy-done.1
  27.3 1.7 copy.28
  29.0 100.8 %reduce-scatter.2.cloned.1.call-done = f32[896,512]{0,1:T(8,128)} async-done(((f32[7168,512]{0,1:T(8,128)}), f32[896,512]{0,1:T(8,128)}) %reduce-scatter.2.cloned.1.call-update) | async-done | bytes 1835024 | tf_op jit(solution)/shard_map/reduce_scatter | solution.py:41
  129.8 6.9 %fusion.7 = (bf16[896,512]{0,1:T(8,128)(2,1)}, f32[896,512]{0,1:T(8,128)}, f32[896,512]{0,1:T(8,128)}, f32[896,512]{0,1:T(8,128)S(1)}) fusion(f32[896,512]{0,1:T(8,128)} %copy.28, f32[896,512]{0,1:T(8,128)} %reduce-scatter.2.cloned.1.call-done, f32[896,512]{0,1:T(8,128)} %copy.25, f32[896,512]{0,1:T(8,128)} %copy.26), kind=kLoop, calls=%fused_computation.14 | loop fusion | flops 7340032 | bytes 13762560 | tf_op jit(solution)/shard_map/convert_element_type | solution.py:53
  136.7 0.0 all-gather.4.cloned.1.call-update
  136.7 0.0 all-gather.6.cloned.1.call-done
  136.8 2.6 %reduce_sum.9 = f32[14336]{0:T(1024)S(1)} reduce(f32[32,1,14336]{2,1,0:T(1,128)} %all-gather.6.cloned.1.call-done, f32[]{:T(128)} %constant.5.clone.1), dimensions={0,1}, to_apply=%region_1.2 | reduce | flops 444416 | bytes 1892356 | tf_op jit(solution)/shard_map/reduce_sum | solution.py:50
  139.3 0.0 copy-done.2
  139.3 0.0 copy-done.3
  139.4 0.7 multiply_subtract_fusion.1
  140.0 2.7 %copy.30 = f32[896,512]{1,0:T(8,128)} copy(f32[896,512]{0,1:T(8,128)} %get-tuple-element.25) | data formatting | bytes 3670016
  142.8 2.9 %copy.31 = f32[896,512]{1,0:T(8,128)} copy(f32[896,512]{0,1:T(8,128)} %get-tuple-element.26) | data formatting | bytes 3670016
  145.6 1.7 copy.32
  147.3 39.0 %all-gather.4.cloned.1.call-done = bf16[7168,512]{0,1:T(8,128)(2,1)} async-done(((bf16[896,512]{0,1:T(8,128)(2,1)}), bf16[7168,512]{0,1:T(8,128)(2,1)}) %all-gather.4.cloned.1.call-update) | async-done | bytes 7340048 | tf_op jit(solution)/shard_map/all_gather | solution.py:53
  186.4 10.4 %copy.29 = bf16[7168,512]{1,0:T(8,128)(2,1)} copy(bf16[7168,512]{0,1:T(8,128)(2,1)} %all-gather.4.cloned.1.call-done) | data formatting | bytes 14680064
  (7 shorter events, 0.0 us)
Async XLA Ops:
  8.0 121.8 %reduce-scatter.2.cloned.1.call-start = ((), (), s32[]{:S(2)}) async-start(), calls=%async_computation.1 | async-start | bytes 16515072 | tf_op jit(solution)/shard_map/reduce_scatter | solution.py:41
  21.3 1.5 copy-start
  21.3 115.4 %all-gather.6.cloned.1.call-start = ((), (), s32[]{:S(2)}) async-start(), calls=%async_computation.3 | async-start | bytes 1892352 | tf_op jit(solution)/shard_map/all_gather | solution.py:49
  21.9 164.5 %all-gather.4.cloned.1.call-start = ((), (), s32[]{:S(2)}) async-start(), calls=%async_computation.2 | async-start | bytes 8257536 | tf_op jit(solution)/shard_map/all_gather | solution.py:53
  24.5 2.9 %copy-start.1 = (f32[896,512]{1,0:T(8,128)S(1)}, f32[896,512]{1,0:T(8,128)}, u32[]{:S(2)}) copy-start(f32[896,512]{1,0:T(8,128)} %param.13) | copy-start | bytes 5505028
  136.7 2.6 %copy-start.2 = (f32[14336]{0:T(1024)S(1)}, f32[14336]{0:T(1024)}, u32[]{:S(2)}) copy-start(f32[14336]{0:T(1024)} %param.17) | copy-start | bytes 172036
  136.7 2.6 %copy-start.3 = (f32[14336]{0:T(1024)S(1)}, f32[14336]{0:T(1024)}, u32[]{:S(2)}) copy-start(f32[14336]{0:T(1024)} %param.18) | copy-start | bytes 172036
  136.7 2.6 %copy-start.4 = (f32[14336]{0:T(1024)S(1)}, f32[14336]{0:T(1024)}, u32[]{:S(2)}) copy-start(f32[14336]{0:T(1024)} %param.19) | copy-start | bytes 172036
Sparse Core Ops, SparseCore 0:
  21.4 108.3 reduce-scatter.1
Sparse Core Ops, SparseCore 1:
  24.6 73.8 all-gather.5
  136.8 49.5 all-gather.3
